TPU v7x, 32 devices: a whole 2x2x4 slice. The times are simulated.
32 devices in a mesh: seq: 8 (over z, y), tp: 4 (over x, core).
Axes of the slice: x: 2, y: 2, z: 4, core: 2. Of those that a mesh axis runs over, the one named last changes fastest.
Arguments:
- inputs: bfloat16 [2, 32, 8192], P(None, 'seq', 'tp'), may hold values from -6 to 6
- out_grad: bfloat16 [2, 32, 8192], P(None, 'seq', 'tp'), may hold values from -6 to 6
- gate_weight: bfloat16 [8192, 14848], P('tp', 'seq'), may hold values from -0.0625 to 0.0625
- up_weight: bfloat16 [8192, 14848], P('tp', 'seq'), may hold values from -0.0625 to 0.0625
- down_weight: bfloat16 [14848, 8192], P('seq', 'tp'), may hold values from -0.0625 to 0.0625
Outputs:
- input_grad: bfloat16 [2, 32, 8192], P(None, 'seq', 'tp')
- gate_grad: float32 [8192, 14848], P('tp', 'seq')
- up_grad: float32 [8192, 14848], P('tp', 'seq')
- down_grad: float32 [14848, 8192], P('seq', 'tp')
All inputs are finite; a program needn't handle non-finite values.
Results may differ from a plain program's by a relative error of at most 0.0049.
Values may be sent and summed in bfloat16 or wider, within the bound.
A program may use at most 128 MiB of HBM per device.

v0:
```python
import jax
import jax.numpy as jnp
from jax import lax
from jax.sharding import PartitionSpec as P


def per_device(inputs, out_grad, gate_weight, up_weight, down_weight):
    blocks = inputs.shape[0]
    local_rows = inputs.shape[1]
    width_count = lax.axis_size("tp")
    block_tokens = local_rows * lax.axis_size("seq")
    share_rows = block_tokens // width_count
    share_start = lax.axis_index("tp") * share_rows
    contract_first = (((0,), (0,)), ((), ()))
    contract_last = (((1,), (1,)), ((), ()))
    totals = None
    results = [None] * blocks
    for index in range(blocks):
        whole_in = lax.all_gather(inputs[index], "seq", axis=0, tiled=True)
        whole_grad = lax.all_gather(out_grad[index], "seq", axis=0, tiled=True)
        gate_part = jnp.dot(whole_in, gate_weight, preferred_element_type=jnp.float32)
        up_part = jnp.dot(whole_in, up_weight, preferred_element_type=jnp.float32)
        gate, up_proj = lax.psum((gate_part, up_part), "tp")
        hidden_share = lax.psum_scatter(
            lax.dot_general(
                whole_grad, down_weight, contract_last, preferred_element_type=jnp.float32
            ),
            "tp",
            scatter_dimension=0,
            tiled=True,
        )
        gate_share = lax.dynamic_slice_in_dim(gate, share_start, share_rows, 0)
        up_share = lax.dynamic_slice_in_dim(up_proj, share_start, share_rows, 0)
        sig = jax.nn.sigmoid(gate_share)
        up_local = (hidden_share * gate_share * sig).astype(jnp.bfloat16)
        gate_local = (hidden_share * up_share * sig * (1.0 + gate_share * (1.0 - sig))).astype(
            jnp.bfloat16
        )
        front_unit_gate = lax.all_gather(gate_local, "tp", axis=0, tiled=True)
        front_unit_up = lax.all_gather(up_local, "tp", axis=0, tiled=True)
        hidden = (jax.nn.silu(gate) * up_proj).astype(jnp.bfloat16)
        down_term = lax.dot_general(
            hidden, whole_grad, contract_first, preferred_element_type=jnp.float32
        )
        gate_term = lax.dot_general(
            whole_in, front_unit_gate, contract_first, preferred_element_type=jnp.float32
        )
        up_term = lax.dot_general(
            whole_in, front_unit_up, contract_first, preferred_element_type=jnp.float32
        )
        terms = (gate_term, up_term, down_term)
        if totals is None:
            totals = terms
        else:
            totals = (totals[0] + terms[0], totals[1] + terms[1], totals[2] + terms[2])
        first = lax.dot_general(
            front_unit_gate, gate_weight, contract_last, preferred_element_type=jnp.float32
        )
        second = lax.dot_general(
            front_unit_up, up_weight, contract_last, preferred_element_type=jnp.float32
        )
        results[index] = lax.psum_scatter(
            first + second, "seq", scatter_dimension=0, tiled=True
        ).astype(jnp.bfloat16)
    return (jnp.stack(results), totals[0], totals[1], totals[2])


def solution(mesh):
    return jax.shard_map(
        per_device,
        mesh=mesh,
        in_specs=(
            P(None, "seq", "tp"),
            P(None, "seq", "tp"),
            P("tp", "seq"),
            P("tp", "seq"),
            P("seq", "tp"),
        ),
        out_specs=(P(None, "seq", "tp"), P("tp", "seq"), P("tp", "seq"), P("seq", "tp")),
        check_vma=False,
    )
```

profile of v0, /device:TPU:0, one launch (start us, length us, event | category | flops | bytes accessed | tf_op | source)
XLA Modules:
  0.0 335.3 jit_solution(6774601214005411477)
XLA Ops:
  8.2 32.8 %all-gather.3 = bf16[1,32,2048]{2,0,1:T(2,128)(2,1)S(1)} all-gather(bf16[1,4,2048]{2,0,1:T(2,128)(2,1)S(1)} %copy.24), channel_id=5, replica_groups=mesh['seq'=8,'tp'=4] {'seq'}, dimensions={1}, use_global_device_ids=true | all-gather | bytes 147456 | tf_op jit(solution)/shard_map/all_gather | solution.py:19
  41.1 30.7 %all-gather.1 = bf16[1,32,2048]{2,0,1:T(2,128)(2,1)S(1)} all-gather(bf16[1,4,2048]{2,0,1:T(2,128)(2,1)S(1)} %copy.22), channel_id=3, replica_groups=mesh['seq'=8,'tp'=4] {'seq'}, dimensions={1}, use_global_device_ids=true | all-gather | bytes 147456 | tf_op jit(solution)/shard_map/all_gather | solution.py:19
  71.9 6.4 %fusion.13 = f32[32,1856]{1,0:T(8,128)} fusion(bf16[2048,1856]{0,1:T(8,128)(2,1)} %param.7, bf16[1,32,2048]{2,1,0:T(8,128)(2,1)S(1)} %copy.18), kind=kOutput, calls=%fused_computation.20 | convolution fusion | flops 243269632 | bytes 7970816 | tf_op jit(solution)/shard_map/dot_general | solution.py:21
  78.3 3.0 fusion.15
  81.4 3.0 fusion.2
  84.4 3.0 fusion.4
  87.5 30.7 %all-gather.2 = bf16[1,32,2048]{2,0,1:T(2,128)(2,1)S(1)} all-gather(bf16[1,4,2048]{2,0,1:T(2,128)(2,1)S(1)} %copy.23), channel_id=4, replica_groups=mesh['seq'=8,'tp'=4] {'seq'}, dimensions={1}, use_global_device_ids=true | all-gather | bytes 147456 | tf_op jit(solution)/shard_map/all_gather | solution.py:20
  118.3 32.9 %all-gather = bf16[1,32,2048]{2,0,1:T(2,128)(2,1)} all-gather(bf16[1,4,2048]{2,0,1:T(2,128)(2,1)S(1)} %copy.21), channel_id=2, replica_groups=mesh['seq'=8,'tp'=4] {'seq'}, dimensions={1}, use_global_device_ids=true | all-gather | bytes 147456 | tf_op jit(solution)/shard_map/all_gather | solution.py:20
  151.2 4.0 %fusion.19 = f32[32,1856]{1,0:T(8,128)} fusion(bf16[1856,2048]{1,0:T(8,128)(2,1)S(1)} %bitcast.63, bf16[1,32,2048]{2,0,1:T(2,128)(2,1)} %all-gather), kind=kOutput, calls=%fused_computation.26 | convolution fusion | flops 243269632 | bytes 7970816 | tf_op jit(solution)/shard_map/dot_general | solution.py:25
  155.2 3.0 fusion.7
  160.8 40.2 %all-reduce.9.cloned.1.call-done = (f32[32,1856]{1,0:T(8,128)}, f32[32,1856]{1,0:T(8,128)}, f32[32,1856]{1,0:T(8,128)}, f32[32,1856]{1,0:T(8,128)}, f32[32,1856]{1,0:T(8,128)}, /*index=5*/f32[32,1856]{1,0:T(8,128)}) async-done(((f32[32,1856]{1,0:T(8,128)}, f32[32,1856]{1,0:T(8,128)}, f32[32,1856]{1,0:T(8,128)}, f32[32,1856]{1,0:T(8,128)}, f32[32,1856]{1,0:T(8,128)}, /*index=5*/f32[32,1856]{1,0:T(8,128)}), ...) | async-done | bytes 1425424 | tf_op jit(solution)/shard_map/psum | solution.py:23
  201.0 3.5 %fusion.17 = f32[1856,2048]{1,0:T(8,128)S(1)} fusion(f32[32,1856]{1,0:T(8,128)} %get-tuple-element.9, f32[32,1856]{1,0:T(8,128)} %get-tuple-element.11, bf16[1,32,2048]{2,0,1:T(2,128)(2,1)} %all-gather), kind=kOutput, calls=%fused_computation.24 | convolution fusion | flops 243625984 | bytes 15810560 | tf_op jit(solution)/shard_map/dot_general | solution.py:42
  205.5 5.4 %all_gather.26 = bf16[32,1856]{1,0:T(8,128)(2,1)S(1)} all-gather(bf16[8,1856]{1,0:T(8,128)(2,1)S(1)} %get-tuple-element.13), channel_id=1, replica_groups=mesh['seq'=8,'tp'=4] {'tp'}, dimensions={0}, use_global_device_ids=true | all-gather | bytes 148480 | tf_op jit(solution)/shard_map/all_gather | solution.py:39
  212.3 7.8 %fusion.11 = f32[1856,2048]{1,0:T(8,128)} fusion(bf16[32,1856]{1,0:T(8,128)(2,1)S(1)} %all_gather.26, bf16[1,32,2048]{2,1,0:T(8,128)(2,1)S(1)} %copy-done.2), kind=kOutput, calls=%fused_computation.18 | convolution fusion | flops 243269632 | bytes 15454208 | tf_op jit(solution)/shard_map/dot_general | solution.py:45
  221.0 5.5 %all_gather.31 = bf16[32,1856]{1,0:T(8,128)(2,1)S(1)} all-gather(bf16[8,1856]{1,0:T(8,128)(2,1)S(1)} %get-tuple-element.14), channel_id=1, replica_groups=mesh['seq'=8,'tp'=4] {'tp'}, dimensions={0}, use_global_device_ids=true | all-gather | bytes 148480 | tf_op jit(solution)/shard_map/all_gather | solution.py:40
  226.5 5.4 %all_gather.27 = bf16[32,1856]{1,0:T(8,128)(2,1)S(1)} all-gather(bf16[8,1856]{1,0:T(8,128)(2,1)S(1)} %get-tuple-element.12), channel_id=1, replica_groups=mesh['seq'=8,'tp'=4] {'tp'}, dimensions={0}, use_global_device_ids=true | all-gather | bytes 148480 | tf_op jit(solution)/shard_map/all_gather | solution.py:40
  231.9 5.6 %all_gather.30 = bf16[32,1856]{1,0:T(8,128)(2,1)S(1)} all-gather(bf16[8,1856]{1,0:T(8,128)(2,1)S(1)} %get-tuple-element.15), channel_id=1, replica_groups=mesh['seq'=8,'tp'=4] {'tp'}, dimensions={0}, use_global_device_ids=true | all-gather | bytes 148480 | tf_op jit(solution)/shard_map/all_gather | solution.py:39
  237.5 7.8 %fusion.9 = f32[1856,2048]{1,0:T(8,128)} fusion(bf16[32,1856]{1,0:T(8,128)(2,1)S(1)} %all_gather.27, bf16[1,32,2048]{2,1,0:T(8,128)(2,1)S(1)} %copy-done.2), kind=kOutput, calls=%fused_computation.16 | convolution fusion | flops 243269632 | bytes 15454208 | tf_op jit(solution)/shard_map/dot_general | solution.py:48
  245.3 2.1 convolution_add_fusion.2
  248.9 1.4 convolution_add_fusion.1
  250.3 7.8 %convolution_add_fusion = f32[1856,2048]{1,0:T(8,128)} fusion(f32[1856,2048]{1,0:T(8,128)S(1)} %fusion.17, f32[32,1856]{1,0:T(8,128)S(1)} %copy-done.6, f32[32,1856]{1,0:T(8,128)S(1)} %copy-done.7, bf16[1,32,2048]{2,0,1:T(2,128)(2,1)S(1)} %copy-done.4), kind=kOutput, calls=%fused_computation.2 | convolution fusion | flops 247427072 | bytes 31014912 | tf_op jit(solution)/shard_map/dot_general | solution.py:42
  258.2 13.1 %add_bitcast_fusion = f32[2048,1856]{0,1:T(8,128)} fusion(f32[1856,2048]{1,0:T(8,128)} %fusion.9, bf16[32,1856]{1,0:T(8,128)(2,1)S(1)} %all_gather.31, bf16[1,32,2048]{2,1,0:T(8,128)(2,1)S(1)} %copy.20), kind=kOutput, calls=%fused_computation | convolution fusion | flops 247070720 | bytes 30658560 | tf_op jit(solution)/shard_map/dot_general | solution.py:48
  271.3 13.2 %add_bitcast_fusion.1 = f32[2048,1856]{0,1:T(8,128)} fusion(f32[1856,2048]{1,0:T(8,128)} %fusion.11, bf16[32,1856]{1,0:T(8,128)(2,1)S(1)} %all_gather.30, bf16[1,32,2048]{2,1,0:T(8,128)(2,1)S(1)} %copy.20), kind=kOutput, calls=%fused_computation.1 | convolution fusion | flops 247070720 | bytes 30658560 | tf_op jit(solution)/shard_map/dot_general | solution.py:45
  284.5 43.3 %all-reduce.10 = (bf16[32,2048]{1,0:T(8,128)(2,1)S(1)}, bf16[32,2048]{1,0:T(8,128)(2,1)S(1)}) all-reduce(f32[32,2048]{1,0:T(8,128)S(1)} %convolution_add_fusion.1, f32[32,2048]{1,0:T(8,128)S(1)} %copy-done.5), channel_id=9, replica_groups=mesh['seq'=8,'tp'=4] {'seq'}, use_global_device_ids=true, to_apply=%region_7.8.clone | all-reduce | flops 131072 | bytes 786432
  (60 shorter events, 7.8 us)
Async XLA Ops:
  7.2 193.8 %all-reduce.9.cloned.1.call-start = ((), (), s32[]{:S(2)}) async-start(), calls=%async_computation | async-start | bytes 2949120 | tf_op jit(solution)/shard_map/psum | solution.py:23
  7.2 71.1 %copy-start = (bf16[2048,1856]{0,1:T(8,128)(2,1)S(1)}, bf16[2048,1856]{0,1:T(8,128)(2,1)}, u32[]{:S(2)}) copy-start(bf16[2048,1856]{0,1:T(8,128)(2,1)} %param.8) | copy-start | bytes 22806532
  71.9 6.4 %copy-start.1 = (bf16[1,32,2048]{2,1,0:T(8,128)(2,1)}, bf16[1,32,2048]{2,1,0:T(8,128)(2,1)S(1)}, u32[]{:S(2)}) copy-start(bf16[1,32,2048]{2,1,0:T(8,128)(2,1)S(1)} %copy.18) | copy-start | bytes 393220
  71.9 9.4 %slice-start = ((s8[7602176]{0:T(1024)(128)(4,1)}), s8[4194304]{0:T(1024)(128)(4,1)S(1)}, s32[]{:S(2)}) async-start(s8[7602176]{0:T(1024)(128)(4,1)} %bitcast.56), calls=%async_computation.1 | async-start | bytes 8388608
  78.3 3.0 slice-start.1
  81.3 6.1 %copy-start.8 = (bf16[2,4,2048]{2,1,0:T(4,128)(2,1)S(1)}, bf16[2,4,2048]{2,1,0:T(4,128)(2,1)}, u32[]{:S(2)}) copy-start(bf16[2,4,2048]{2,1,0:T(4,128)(2,1)} %param.6) | copy-start | bytes 98308
  81.3 69.8 %slice-start.6 = ((s8[7602176]{0:T(1024)(128)(4,1)}), s8[4194304]{0:T(1024)(128)(4,1)S(1)}, s32[]{:S(2)}) async-start(s8[7602176]{0:T(1024)(128)(4,1)} %bitcast.62), calls=%async_computation.7 | async-start | bytes 8388608
  84.4 66.8 %slice-start.7 = ((s8[7602176]{0:T(1024)(128)(4,1)}), s8[3407872]{0:T(1024)(128)(4,1)S(1)}, s32[]{:S(2)}) async-start(s8[7602176]{0:T(1024)(128)(4,1)} %bitcast.62), calls=%async_computation.8 | async-start | bytes 6815744
  118.3 37.0 %copy-start.3 = (bf16[1,32,2048]{2,0,1:T(2,128)(2,1)}, bf16[1,32,2048]{2,0,1:T(2,128)(2,1)S(1)}, u32[]{:S(2)}) copy-start(bf16[1,32,2048]{2,0,1:T(2,128)(2,1)S(1)} %all-gather.2) | copy-start | bytes 393220
  151.2 7.1 %copy-start.10 = (u32[32]{0:T(128)S(1)}, u32[32]{0:T(128)}, u32[]{:S(2)}) copy-start(u32[32]{0:T(128)} %constant.23) | copy-start | bytes 388
  151.2 7.8 %copy-start.9 = (u32[32]{0:T(128)S(1)}, u32[32]{0:T(128)}, u32[]{:S(2)}) copy-start(u32[32]{0:T(128)} %constant.19) | copy-start | bytes 388
  158.3 52.6 %slice-start.2 = ((s8[7602176]{0:T(1024)(128)(4,1)}), s8[3407872]{0:T(1024)(128)(4,1)S(1)}, s32[]{:S(2)}) async-start(s8[7602176]{0:T(1024)(128)(4,1)} %bitcast.58), calls=%async_computation.3 | async-start | bytes 6815744
  201.0 9.9 %slice-start.3 = ((s8[7602176]{0:T(1024)(128)(4,1)}), s8[4194304]{0:T(1024)(128)(4,1)S(1)}, s32[]{:S(2)}) async-start(s8[7602176]{0:T(1024)(128)(4,1)} %bitcast.58), calls=%async_computation.4 | async-start | bytes 8388608
  210.9 1.4 copy-start.2
  212.3 7.8 %copy-start.6 = (f32[32,1856]{1,0:T(8,128)S(1)}, f32[32,1856]{1,0:T(8,128)}, u32[]{:S(2)}) copy-start(f32[32,1856]{1,0:T(8,128)} %get-tuple-element.6) | copy-start | bytes 712708
  212.3 7.8 %copy-start.7 = (f32[32,1856]{1,0:T(8,128)S(1)}, f32[32,1856]{1,0:T(8,128)}, u32[]{:S(2)}) copy-start(f32[32,1856]{1,0:T(8,128)} %get-tuple-element.8) | copy-start | bytes 712708
  212.3 33.0 %slice-start.4 = ((s8[7602176]{0:T(1024)(128)(4,1)}), s8[4194304]{0:T(1024)(128)(4,1)S(1)}, s32[]{:S(2)}) async-start(s8[7602176]{0:T(1024)(128)(4,1)} %bitcast.60), calls=%async_computation.5 | async-start | bytes 8388608
  221.0 24.3 %slice-start.5 = ((s8[7602176]{0:T(1024)(128)(4,1)}), s8[3407872]{0:T(1024)(128)(4,1)S(1)}, s32[]{:S(2)}) async-start(s8[7602176]{0:T(1024)(128)(4,1)} %bitcast.60), calls=%async_computation.6 | async-start | bytes 6815744
  248.9 1.5 copy-start.4
  271.3 13.2 %copy-start.5 = (f32[32,2048]{1,0:T(8,128)S(1)}, f32[32,2048]{1,0:T(8,128)}, u32[]{:S(2)}) copy-start(f32[32,2048]{1,0:T(8,128)} %convolution_add_fusion.2) | copy-start | bytes 786436
Sparse Core Ops, SparseCore 0:
  158.4 42.5 all-reduce.8
where the time goes:
time: 336 us; the launch traced here: 335 us
  blocking collectives  192 us (57%)
  matrix products  82.2 us (24%)
  waiting for transfers between devices  40.2 us (12%)
  between operations  15.5 us (5%)
    all_gather x2, blocking collectives, per_device(): whole_grad = lax.all_gather(out_grad[index], 'seq', axis=0, tiled=True)  63.7 us
    all_gather x2, blocking collectives, per_device(): whole_in = lax.all_gather(inputs[index], 'seq', axis=0, tiled=True)  63.6 us
    unnamed x1, blocking collectives  43.3 us
    psum x1, waiting for transfers between devices, per_device(): gate, up_proj = lax.psum((gate_part, up_part), 'tp')  40.2 us
    dot_general x2, matrix products, per_device(): lax.dot_general(whole_in, front_unit_gate, contract_first, preferred_elem...  21 us
    dot_general x2, matrix products, per_device(): lax.dot_general(whole_in, front_unit_up, contract_first, preferred_elemen...  20.9 us
    dot_general x2, matrix products, per_device(): lax.dot_general(hidden, whole_grad, contract_first, preferred_element_typ...  11.4 us
    all_gather x2, blocking collectives, per_device(): front_unit_gate = lax.all_gather(gate_local, 'tp', axis=0, tiled=True)  11 us
  transfers between devices with their start and end apart: 1, of which 1 were waited for; matrix products, arithmetic and copies ran while one was open for 0% of the time, Pallas kernels for 0%

commit v1 on v0

--- a/solution.py
+++ b/solution.py
@@ -17,7 +17,14 @@
     results = [None] * blocks
     for index in range(blocks):
         whole_in = lax.all_gather(inputs[index], "seq", axis=0, tiled=True)
-        whole_grad = lax.all_gather(out_grad[index], "seq", axis=0, tiled=True)
+        ring = [out_grad[index]]
+        for hop in range(7):
+            ring.append(lax.ppermute(ring[-1], "seq", [(dev, (dev + 1) % 8) for dev in range(8)]))
+        whole_grad = jnp.roll(
+            jnp.concatenate(ring[::-1], axis=0),
+            (lax.axis_index("seq") + 1) * ring[0].shape[0],
+            axis=0,
+        )
         gate_part = jnp.dot(whole_in, gate_weight, preferred_element_type=jnp.float32)
         up_part = jnp.dot(whole_in, up_weight, preferred_element_type=jnp.float32)
         gate, up_proj = lax.psum((gate_part, up_part), "tp")

time: 336 us -> 301 us (0.90)
  blocking collectives: 192 us -> 128 us
  waiting for transfers between devices: 40.2 us -> 53.8 us
  starting transfers between devices: 0.04 us -> 8.88 us
  matrix products: 82.2 us -> 88.4 us
    all_gather x2 -> x0, blocking collectives: 63.7 us -> none  [per_device(): whole_grad = lax.all_gather(out_grad[index], 'seq', axis=0, tiled=True)]
    ppermute x0 -> x14, waiting for transfers between devices: none -> 13.7 us  [per_device(): lax.ppermute(ring[-1], 'seq', [(dev, (dev + 1) % 8) for dev in range(8)])]
    ppermute x0 -> x14, starting transfers between devices: none -> 8.84 us  [per_device(): lax.ppermute(ring[-1], 'seq', [(dev, (dev + 1) % 8) for dev in range(8)])]
    dot_general x2, matrix products: 7.05 us -> 12.4 us  [per_device(): lax.dot_general(whole_grad, down_weight, contract_last, preferred_element...]
  transfers between devices with their start and end apart: 1 -> 15, of which waited for: 1 -> 7; matrix products, arithmetic and copies ran while one was open for 0% -> 8% of each run, Pallas kernels for 0% -> 0%
where the time goes in v1:
time: 301 us
  blocking collectives  128 us (43%)
  matrix products  88.4 us (29%)
  waiting for transfers between devices  53.8 us (18%)
  between operations  15.4 us (5%)
  starting transfers between devices  8.88 us (3%)
  local copies, waits for them, and re-layouts  3.36 us (1%)
    all_gather x2, blocking collectives, per_device(): whole_in = lax.all_gather(inputs[index], 'seq', axis=0, tiled=True)  63 us
    unnamed x1, blocking collectives  43.3 us
    psum x1, waiting for transfers between devices, per_device(): gate, up_proj = lax.psum((gate_part, up_part), 'tp')  40.1 us
    dot_general x2, matrix products, per_device(): lax.dot_general(whole_in, front_unit_gate, contract_first, preferred_elem...  20.9 us
    dot_general x2, matrix products, per_device(): lax.dot_general(whole_in, front_unit_up, contract_first, preferred_elemen...  20.9 us
    ppermute x14, waiting for transfers between devices, per_device(): lax.ppermute(ring[-1], 'seq', [(dev, (dev + 1) % 8) for dev in range(8)])  13.7 us
    dot_general x2, matrix products, per_device(): lax.dot_general(whole_grad, down_weight, contract_last, preferred_element...  12.4 us
    all_gather x2, blocking collectives, per_device(): front_unit_gate = lax.all_gather(gate_local, 'tp', axis=0, tiled=True)  11 us
  transfers between devices with their start and end apart: 15, of which 7 were waited for; matrix products, arithmetic and copies ran while one was open for 8% of the time, Pallas kernels for 0%

profile of v1, /device:TPU:0, one launch (start us, length us, event | category | flops | bytes accessed | tf_op | source)
XLA Modules:
  0.0 300.5 jit_solution(7183698968443532285)
XLA Ops:
  8.1 3.0 %collective-permute-start = (bf16[4,2048]{1,0:T(4,128)(2,1)S(1)}, bf16[4,2048]{1,0:T(4,128)(2,1)S(1)}, u32[]{:S(2)}, u32[]{:S(2)}) collective-permute-start(bf16[4,2048]{1,0:T(4,128)(2,1)S(1)} %get-tuple-element.17), channel_id=1, source_target_pairs={{0,4},{4,8},{8,12},{12,16},{16,20},{20,24},{24,28},{28,0},{1,5},{5... | collective-permute-start | bytes 49160 | tf_op jit(solution)/shard_map/ppermute | solution.py:22
  13.5 4.1 %collective-permute-done.7 = bf16[4,2048]{1,0:T(4,128)(2,1)S(1)} collective-permute-done((bf16[4,2048]{1,0:T(4,128)(2,1)S(1)}, bf16[4,2048]{1,0:T(4,128)(2,1)S(1)}, u32[]{:S(2)}, u32[]{:S(2)}) %collective-permute-start.7) | collective-permute-done | bytes 16416 | tf_op jit(solution)/shard_map/ppermute | solution.py:22
  17.6 30.9 %all-gather = bf16[1,32,2048]{2,0,1:T(2,128)(2,1)S(1)} all-gather(bf16[1,4,2048]{2,0,1:T(2,128)(2,1)S(1)} %copy.15), channel_id=2, replica_groups=mesh['seq'=8,'tp'=4] {'seq'}, dimensions={1}, use_global_device_ids=true | all-gather | bytes 147456 | tf_op jit(solution)/shard_map/all_gather | solution.py:19
  50.8 6.2 %fusion.12 = f32[32,1856]{1,0:T(8,128)} fusion(bf16[2048,1856]{0,1:T(8,128)(2,1)} %param.9, bf16[1,32,2048]{2,1,0:T(8,128)(2,1)S(1)} %copy.13), kind=kOutput, calls=%fused_computation.23 | convolution fusion | flops 243269632 | bytes 7970816 | tf_op jit(solution)/shard_map/dot_general | solution.py:28
  57.5 3.1 %fusion.14 = f32[32,1856]{1,0:T(8,128)} fusion(bf16[2048,1856]{0,1:T(8,128)(2,1)S(1)} %copy-done, bf16[1,32,2048]{2,1,0:T(8,128)(2,1)S(1)} %copy.13), kind=kOutput, calls=%fused_computation.25 | convolution fusion | flops 243269632 | bytes 7970816 | tf_op jit(solution)/shard_map/dot_general | solution.py:29
  60.6 2.8 collective-permute-done.2
  64.2 32.0 %all-gather.1 = bf16[1,32,2048]{2,0,1:T(2,128)(2,1)S(1)} all-gather(bf16[1,4,2048]{2,0,1:T(2,128)(2,1)S(1)} %copy.16), channel_id=3, replica_groups=mesh['seq'=8,'tp'=4] {'seq'}, dimensions={1}, use_global_device_ids=true | all-gather | bytes 147456 | tf_op jit(solution)/shard_map/all_gather | solution.py:19
  97.2 3.0 %fusion.4 = f32[32,1856]{1,0:T(8,128)} fusion(bf16[2048,1856]{0,1:T(8,128)(2,1)S(1)} %bitcast.51, bf16[1,32,2048]{2,1,0:T(8,128)(2,1)S(1)} %copy.14), kind=kOutput, calls=%fused_computation.15 | convolution fusion | flops 243269632 | bytes 7970816 | tf_op jit(solution)/shard_map/dot_general | solution.py:28
  103.5 3.0 %fusion.6 = f32[32,1856]{1,0:T(8,128)} fusion(bf16[2048,1856]{0,1:T(8,128)(2,1)S(1)} %copy-done, bf16[1,32,2048]{2,1,0:T(8,128)(2,1)S(1)} %copy.14), kind=kOutput, calls=%fused_computation.17 | convolution fusion | flops 243269632 | bytes 7970816 | tf_op jit(solution)/shard_map/dot_general | solution.py:29
  106.6 2.7 collective-permute-done.5
  110.1 6.2 %fusion.26 = f32[32,1856]{1,0:T(8,128)} fusion(bf16[1856,2048]{1,0:T(8,128)(2,1)} %param.11, s32[]{:T(128)S(6)} %select_n.20, bf16[32,2048]{1,0:T(8,128)(2,1)S(1)} %concatenate.10), kind=kOutput, calls=%fused_computation.46 | convolution fusion | flops 243531776 | bytes 7970820 | tf_op jit(solution)/shard_map/dot_general | solution.py:32
  116.5 6.2 %fusion.23 = f32[32,1856]{1,0:T(8,128)} fusion(bf16[1856,2048]{1,0:T(8,128)(2,1)} %param.11, s32[]{:T(128)S(6)} %select_n.20, bf16[32,2048]{1,0:T(8,128)(2,1)S(1)} %concatenate.9), kind=kOutput, calls=%fused_computation.45 | convolution fusion | flops 243531776 | bytes 7970820 | tf_op jit(solution)/shard_map/dot_general | solution.py:32
  125.1 40.1 %all-reduce.9.cloned.1.call-done = (f32[32,1856]{1,0:T(8,128)}, f32[32,1856]{1,0:T(8,128)}, f32[32,1856]{1,0:T(8,128)}, f32[32,1856]{1,0:T(8,128)}, f32[32,1856]{1,0:T(8,128)}, /*index=5*/f32[32,1856]{1,0:T(8,128)}) async-done(((f32[32,1856]{1,0:T(8,128)}, f32[32,1856]{1,0:T(8,128)}, f32[32,1856]{1,0:T(8,128)}, f32[32,1856]{1,0:T(8,128)}, f32[32,1856]{1,0:T(8,128)}, /*index=5*/f32[32,1856]{1,0:T(8,128)}), ...) | async-done | bytes 1425424 | tf_op jit(solution)/shard_map/psum | solution.py:30
  166.1 5.6 %all_gather.19 = bf16[32,1856]{1,0:T(8,128)(2,1)S(1)} all-gather(bf16[8,1856]{1,0:T(8,128)(2,1)S(1)} %get-tuple-element.14), channel_id=1, replica_groups=mesh['seq'=8,'tp'=4] {'tp'}, dimensions={0}, use_global_device_ids=true | all-gather | bytes 148480 | tf_op jit(solution)/shard_map/all_gather | solution.py:46
  171.6 4.6 %fusion.30 = f32[32,2048]{1,0:T(8,128)S(1)} fusion(bf16[32,1856]{1,0:T(8,128)(2,1)S(1)} %all_gather.19, bf16[2048,1856]{0,1:T(8,128)(2,1)} %param.9), kind=kOutput, calls=%fused_computation.48 | convolution fusion | flops 243269632 | bytes 7983104 | tf_op jit(solution)/shard_map/dot_general | solution.py:63
  176.2 7.8 %fusion.10 = f32[1856,2048]{1,0:T(8,128)} fusion(bf16[32,1856]{1,0:T(8,128)(2,1)S(1)} %all_gather.19, bf16[1,32,2048]{2,1,0:T(8,128)(2,1)S(1)} %copy.13), kind=kOutput, calls=%fused_computation.21 | convolution fusion | flops 243269632 | bytes 15454208 | tf_op jit(solution)/shard_map/dot_general | solution.py:52
  187.3 5.4 %all_gather.23 = bf16[32,1856]{1,0:T(8,128)(2,1)S(1)} all-gather(bf16[8,1856]{1,0:T(8,128)(2,1)S(1)} %get-tuple-element.15), channel_id=1, replica_groups=mesh['seq'=8,'tp'=4] {'tp'}, dimensions={0}, use_global_device_ids=true | all-gather | bytes 148480 | tf_op jit(solution)/shard_map/all_gather | solution.py:47
  192.7 5.4 %all_gather.20 = bf16[32,1856]{1,0:T(8,128)(2,1)S(1)} all-gather(bf16[8,1856]{1,0:T(8,128)(2,1)S(1)} %get-tuple-element.13), channel_id=1, replica_groups=mesh['seq'=8,'tp'=4] {'tp'}, dimensions={0}, use_global_device_ids=true | all-gather | bytes 148480 | tf_op jit(solution)/shard_map/all_gather | solution.py:47
  198.1 5.4 %all_gather.22 = bf16[32,1856]{1,0:T(8,128)(2,1)S(1)} all-gather(bf16[8,1856]{1,0:T(8,128)(2,1)S(1)} %get-tuple-element.16), channel_id=1, replica_groups=mesh['seq'=8,'tp'=4] {'tp'}, dimensions={0}, use_global_device_ids=true | all-gather | bytes 148480 | tf_op jit(solution)/shard_map/all_gather | solution.py:46
  203.4 7.8 %fusion.8 = f32[1856,2048]{1,0:T(8,128)} fusion(bf16[32,1856]{1,0:T(8,128)(2,1)S(1)} %all_gather.20, bf16[1,32,2048]{2,1,0:T(8,128)(2,1)S(1)} %copy.13), kind=kOutput, calls=%fused_computation.19 | convolution fusion | flops 243269632 | bytes 15454208 | tf_op jit(solution)/shard_map/dot_general | solution.py:55
  215.6 7.8 %convolution_add_fusion = f32[1856,2048]{1,0:T(8,128)} fusion(f32[1856,2048]{1,0:T(8,128)S(1)} %fusion.16, f32[32,1856]{1,0:T(8,128)S(1)} %copy-done.1, f32[32,1856]{1,0:T(8,128)S(1)} %copy-done.2, s32[]{:T(128)S(6)} %select_n.20, bf16[32,2048]{1,0:T(8,128)(2,1)S(1)} %concatenate.9), kind=kOutput, calls=%fused_computation.2 | convolution fusion | flops 247689216 | bytes 31014916 | tf_op jit(solution)/shard_map/dot_general | solution.py:49
  223.4 13.1 %add_bitcast_fusion = f32[2048,1856]{0,1:T(8,128)} fusion(f32[1856,2048]{1,0:T(8,128)} %fusion.8, bf16[32,1856]{1,0:T(8,128)(2,1)S(1)} %all_gather.23, bf16[1,32,2048]{2,1,0:T(8,128)(2,1)S(1)} %copy.14), kind=kOutput, calls=%fused_computation | convolution fusion | flops 247070720 | bytes 30658560 | tf_op jit(solution)/shard_map/dot_general | solution.py:55
  236.5 13.1 %add_bitcast_fusion.1 = f32[2048,1856]{0,1:T(8,128)} fusion(f32[1856,2048]{1,0:T(8,128)} %fusion.10, bf16[32,1856]{1,0:T(8,128)(2,1)S(1)} %all_gather.22, bf16[1,32,2048]{2,1,0:T(8,128)(2,1)S(1)} %copy.14), kind=kOutput, calls=%fused_computation.1 | convolution fusion | flops 247070720 | bytes 30658560 | tf_op jit(solution)/shard_map/dot_general | solution.py:52
  249.7 43.3 %all-reduce.10 = (bf16[32,2048]{1,0:T(8,128)(2,1)S(1)}, bf16[32,2048]{1,0:T(8,128)(2,1)S(1)}) all-reduce(f32[32,2048]{1,0:T(8,128)S(1)} %convolution_add_fusion.1, f32[32,2048]{1,0:T(8,128)S(1)} %convolution_add_fusion.2), channel_id=7, replica_groups=mesh['seq'=8,'tp'=4] {'seq'}, use_global_device_ids=true, to_apply=%region_7.9.clone | all-reduce | flops 131072 | bytes 786432
  (73 shorter events, 22.3 us)
Async XLA Ops:
  7.2 158.0 %all-reduce.9.cloned.1.call-start = ((), (), s32[]{:S(2)}) async-start(), calls=%async_computation | async-start | bytes 2949120 | tf_op jit(solution)/shard_map/psum | solution.py:30
  7.2 50.3 %copy-start = (bf16[2048,1856]{0,1:T(8,128)(2,1)S(1)}, bf16[2048,1856]{0,1:T(8,128)(2,1)}, u32[]{:S(2)}) copy-start(bf16[2048,1856]{0,1:T(8,128)(2,1)} %param.10) | copy-start | bytes 22806532
  8.1 40.5 %collective-permute-start = (bf16[4,2048]{1,0:T(4,128)(2,1)S(1)}, bf16[4,2048]{1,0:T(4,128)(2,1)S(1)}, u32[]{:S(2)}, u32[]{:S(2)}) collective-permute-start(bf16[4,2048]{1,0:T(4,128)(2,1)S(1)} %get-tuple-element.17), channel_id=1, source_target_pairs={{0,4},{4,8},{8,12},{12,16},{16,20},{20,24},{24,28},{28,0},{1,5},{5... | collective-permute-start | bytes 49160 | tf_op jit(solution)/shard_map/ppermute | solution.py:22
  11.2 6.4 %collective-permute-start.7 = (bf16[4,2048]{1,0:T(4,128)(2,1)S(1)}, bf16[4,2048]{1,0:T(4,128)(2,1)S(1)}, u32[]{:S(2)}, u32[]{:S(2)}) collective-permute-start(bf16[4,2048]{1,0:T(4,128)(2,1)S(1)} %get-tuple-element.18), channel_id=1, source_target_pairs={{0,4},{4,8},{8,12},{12,16},{16,20},{20,24},{24,28},{28,0},{1,5},{5... | collective-permute-start | bytes 49160 | tf_op jit(solution)/shard_map/ppermute | solution.py:22
  17.6 33.1 %collective-permute-start.8 = (bf16[4,2048]{1,0:T(4,128)(2,1)S(1)}, bf16[4,2048]{1,0:T(4,128)(2,1)S(1)}, u32[]{:S(2)}, u32[]{:S(2)}) collective-permute-start(bf16[4,2048]{1,0:T(4,128)(2,1)S(1)} %collective-permute-done.7), channel_id=1, source_target_pairs={{0,4},{4,8},{8,12},{12,16},{16,20},{20,24},{24,28},{28,0},{1,5},{5... | collective-permute-start | bytes 49160 | tf_op jit(solution)/shard_map/ppermute | solution.py:22
  48.6 48.5 %slice-start = ((s8[7602176]{0:T(1024)(128)(4,1)}), s8[4194304]{0:T(1024)(128)(4,1)S(1)}, s32[]{:S(2)}) async-start(s8[7602176]{0:T(1024)(128)(4,1)} %bitcast.50), calls=%async_computation.1 | async-start | bytes 8388608
  48.7 8.3 %collective-permute-start.1 = (bf16[4,2048]{1,0:T(4,128)(2,1)S(1)}, bf16[4,2048]{1,0:T(4,128)(2,1)S(1)}, u32[]{:S(2)}, u32[]{:S(2)}) collective-permute-start(bf16[4,2048]{1,0:T(4,128)(2,1)S(1)} %collective-permute-done), channel_id=1, source_target_pairs={{0,4},{4,8},{8,12},{12,16},{16,20},{20,24},{24,28},{28,0},{1,5},{5... | collective-permute-start | bytes 49160 | tf_op jit(solution)/shard_map/ppermute | solution.py:22
  50.7 6.7 %collective-permute-start.9 = (bf16[4,2048]{1,0:T(4,128)(2,1)S(1)}, bf16[4,2048]{1,0:T(4,128)(2,1)S(1)}, u32[]{:S(2)}, u32[]{:S(2)}) collective-permute-start(bf16[4,2048]{1,0:T(4,128)(2,1)S(1)} %collective-permute-done.8), channel_id=1, source_target_pairs={{0,4},{4,8},{8,12},{12,16},{16,20},{20,24},{24,28},{28,0},{1,5},{5... | collective-permute-start | bytes 49160 | tf_op jit(solution)/shard_map/ppermute | solution.py:22
  56.9 40.2 %slice-start.1 = ((s8[7602176]{0:T(1024)(128)(4,1)}), s8[3407872]{0:T(1024)(128)(4,1)S(1)}, s32[]{:S(2)}) async-start(s8[7602176]{0:T(1024)(128)(4,1)} %bitcast.50), calls=%async_computation.2 | async-start | bytes 6815744
  57.0 6.4 %collective-permute-start.2 = (bf16[4,2048]{1,0:T(4,128)(2,1)S(1)}, bf16[4,2048]{1,0:T(4,128)(2,1)S(1)}, u32[]{:S(2)}, u32[]{:S(2)}) collective-permute-start(bf16[4,2048]{1,0:T(4,128)(2,1)S(1)} %collective-permute-done.1), channel_id=1, source_target_pairs={{0,4},{4,8},{8,12},{12,16},{16,20},{20,24},{24,28},{28,0},{1,5},{5... | collective-permute-start | bytes 49160 | tf_op jit(solution)/shard_map/ppermute | solution.py:22
  57.4 6.7 %collective-permute-start.10 = (bf16[4,2048]{1,0:T(4,128)(2,1)S(1)}, bf16[4,2048]{1,0:T(4,128)(2,1)S(1)}, u32[]{:S(2)}, u32[]{:S(2)}) collective-permute-start(bf16[4,2048]{1,0:T(4,128)(2,1)S(1)} %collective-permute-done.9), channel_id=1, source_target_pairs={{0,4},{4,8},{8,12},{12,16},{16,20},{20,24},{24,28},{28,0},{1,5},{5... | collective-permute-start | bytes 49160 | tf_op jit(solution)/shard_map/ppermute | solution.py:22
  63.4 32.9 %collective-permute-start.3 = (bf16[4,2048]{1,0:T(4,128)(2,1)S(1)}, bf16[4,2048]{1,0:T(4,128)(2,1)S(1)}, u32[]{:S(2)}, u32[]{:S(2)}) collective-permute-start(bf16[4,2048]{1,0:T(4,128)(2,1)S(1)} %collective-permute-done.2), channel_id=1, source_target_pairs={{0,4},{4,8},{8,12},{12,16},{16,20},{20,24},{24,28},{28,0},{1,5},{5... | collective-permute-start | bytes 49160 | tf_op jit(solution)/shard_map/ppermute | solution.py:22
  64.1 33.0 %collective-permute-start.11 = (bf16[4,2048]{1,0:T(4,128)(2,1)S(1)}, bf16[4,2048]{1,0:T(4,128)(2,1)S(1)}, u32[]{:S(2)}, u32[]{:S(2)}) collective-permute-start(bf16[4,2048]{1,0:T(4,128)(2,1)S(1)} %collective-permute-done.10), channel_id=1, source_target_pairs={{0,4},{4,8},{8,12},{12,16},{16,20},{20,24},{24,28},{28,0},{1,5},{5... | collective-permute-start | bytes 49160 | tf_op jit(solution)/shard_map/ppermute | solution.py:22
  96.3 6.5 %collective-permute-start.4 = (bf16[4,2048]{1,0:T(4,128)(2,1)S(1)}, bf16[4,2048]{1,0:T(4,128)(2,1)S(1)}, u32[]{:S(2)}, u32[]{:S(2)}) collective-permute-start(bf16[4,2048]{1,0:T(4,128)(2,1)S(1)} %collective-permute-done.3), channel_id=1, source_target_pairs={{0,4},{4,8},{8,12},{12,16},{16,20},{20,24},{24,28},{28,0},{1,5},{5... | collective-permute-start | bytes 49160 | tf_op jit(solution)/shard_map/ppermute | solution.py:22
  97.1 6.4 %collective-permute-start.12 = (bf16[4,2048]{1,0:T(4,128)(2,1)S(1)}, bf16[4,2048]{1,0:T(4,128)(2,1)S(1)}, u32[]{:S(2)}, u32[]{:S(2)}) collective-permute-start(bf16[4,2048]{1,0:T(4,128)(2,1)S(1)} %collective-permute-done.11), channel_id=1, source_target_pairs={{0,4},{4,8},{8,12},{12,16},{16,20},{20,24},{24,28},{28,0},{1,5},{5... | collective-permute-start | bytes 49160 | tf_op jit(solution)/shard_map/ppermute | solution.py:22
  102.8 6.4 %collective-permute-start.5 = (bf16[4,2048]{1,0:T(4,128)(2,1)S(1)}, bf16[4,2048]{1,0:T(4,128)(2,1)S(1)}, u32[]{:S(2)}, u32[]{:S(2)}) collective-permute-start(bf16[4,2048]{1,0:T(4,128)(2,1)S(1)} %collective-permute-done.4), channel_id=1, source_target_pairs={{0,4},{4,8},{8,12},{12,16},{16,20},{20,24},{24,28},{28,0},{1,5},{5... | collective-permute-start | bytes 49160 | tf_op jit(solution)/shard_map/ppermute | solution.py:22
  103.5 6.4 %collective-permute-start.13 = (bf16[4,2048]{1,0:T(4,128)(2,1)S(1)}, bf16[4,2048]{1,0:T(4,128)(2,1)S(1)}, u32[]{:S(2)}, u32[]{:S(2)}) collective-permute-start(bf16[4,2048]{1,0:T(4,128)(2,1)S(1)} %collective-permute-done.12), channel_id=1, source_target_pairs={{0,4},{4,8},{8,12},{12,16},{16,20},{20,24},{24,28},{28,0},{1,5},{5... | collective-permute-start | bytes 49160 | tf_op jit(solution)/shard_map/ppermute | solution.py:22
  109.2 7.1 %collective-permute-start.6 = (bf16[4,2048]{1,0:T(4,128)(2,1)S(1)}, bf16[4,2048]{1,0:T(4,128)(2,1)S(1)}, u32[]{:S(2)}, u32[]{:S(2)}) collective-permute-start(bf16[4,2048]{1,0:T(4,128)(2,1)S(1)} %collective-permute-done.5), channel_id=1, source_target_pairs={{0,4},{4,8},{8,12},{12,16},{16,20},{20,24},{24,28},{28,0},{1,5},{5... | collective-permute-start | bytes 49160 | tf_op jit(solution)/shard_map/ppermute | solution.py:22
  110.1 12.6 %copy-start.6 = (u32[32]{0:T(128)S(1)}, u32[32]{0:T(128)}, u32[]{:S(2)}) copy-start(u32[32]{0:T(128)} %constant.49) | copy-start | bytes 388
  110.1 13.2 %copy-start.5 = (u32[32]{0:T(128)S(1)}, u32[32]{0:T(128)}, u32[]{:S(2)}) copy-start(u32[32]{0:T(128)} %constant.45) | copy-start | bytes 388
  184.0 27.2 %slice-start.4 = ((s8[7602176]{0:T(1024)(128)(4,1)}), s8[4194304]{0:T(1024)(128)(4,1)S(1)}, s32[]{:S(2)}) async-start(s8[7602176]{0:T(1024)(128)(4,1)} %bitcast.54), calls=%async_computation.5 | async-start | bytes 8388608
  184.0 28.6 %slice-start.2 = ((s8[7602176]{0:T(1024)(128)(4,1)}), s8[3407872]{0:T(1024)(128)(4,1)S(1)}, s32[]{:S(2)}) async-start(s8[7602176]{0:T(1024)(128)(4,1)} %bitcast.52), calls=%async_computation.3 | async-start | bytes 6815744
  186.2 25.0 %slice-start.5 = ((s8[7602176]{0:T(1024)(128)(4,1)}), s8[3407872]{0:T(1024)(128)(4,1)S(1)}, s32[]{:S(2)}) async-start(s8[7602176]{0:T(1024)(128)(4,1)} %bitcast.54), calls=%async_computation.6 | async-start | bytes 6815744
  203.4 9.2 %slice-start.3 = ((s8[7602176]{0:T(1024)(128)(4,1)}), s8[4194304]{0:T(1024)(128)(4,1)S(1)}, s32[]{:S(2)}) async-start(s8[7602176]{0:T(1024)(128)(4,1)} %bitcast.52), calls=%async_computation.4 | async-start | bytes 8388608
  (4 other events, 18.5 us)
Sparse Core Ops, SparseCore 0:
  122.8 42.2 all-reduce.8
